TPU v7x, 256 devices: a whole 4x4x8 slice. The times are simulated.
256 devices in a mesh: blk: 64 (over y, z, core), plane: 4 (over x).
Axes of the slice: x: 4, y: 4, z: 8, core: 2. Of those that a mesh axis runs over, the one named last changes fastest.
Arguments:
- tiles: bfloat16 [1024, 24, 128, 128], P(('blk', 'plane')), may hold values from -0.078125 to 0.078125
- tile_cols: int32 [1024, 24], P(('blk', 'plane')), may hold values from 0 to 511
- tile_count: int32 [1024], P(('blk', 'plane')), may hold values from 18 to 24, as said below
- u_start: float32 [131072], P(('blk', 'plane')), may hold values from -0.015625 to 0.015625
- v_start: float32 [65536], P(('blk', 'plane')), may hold values from -0.0234375 to 0.0234375
- beta_start: float32 [1], replicated, may hold values from 0.5 to 1.5
- left_basis: float32 [131072, 128], P(('blk', 'plane')), may hold values from -0.015625 to 0.015625
- right_basis: float32 [65536, 128], P(('blk', 'plane')), may hold values from -0.0234375 to 0.0234375
Outputs:
- left_vectors: float32 [1, 131072], P(None, ('blk', 'plane'))
- right_vectors: float32 [1, 65536], P(None, ('blk', 'plane'))
- coefficients: float32 [2], replicated
Inputs may be any that keep to these rules, and one draw needn't show every extreme that they name: `tile_count`: slots at and after a row block's count are padding; some row block uses all 24 slots.
All inputs are finite; a program needn't handle non-finite values.
Results may differ from a plain program's by a relative error of at most 0.00055.
The roundings to bfloat16 on the way count: a program that leaves them out, or rounds other values in their place, can miss the bound.
Values may be sent and summed in bfloat16 or wider, within the bound.
A program may use at most 64 MiB of HBM per device.

v0:
```python
import math

import jax
import jax.numpy as jnp
from jax import lax
from jax.sharding import Mesh
from jax.sharding import PartitionSpec as P

BLK_PLANE = ("blk_0", "blk_1", "blk_2", "plane")
BLK = ("blk_0", "blk_1", "blk_2")


def from_everyone(array, axis):
    copies = jnp.broadcast_to(array, (lax.axis_size(axis), *array.shape))
    return lax.all_to_all(copies, axis, split_axis=0, concat_axis=0, tiled=True)


def of_everyone(array, axis):
    return from_everyone(array, axis).sum(axis=0)


def one_axis_at_a_time(array, axes):
    far, near = axes
    nearer = of_everyone(array, near)
    return of_everyone(nearer, far)


def packed_total(arrays, axis):
    ravelled, at, finished = (jnp.concatenate([a.reshape(-1) for a in arrays]), 0, [])
    total = one_axis_at_a_time(ravelled, axis)
    for a in arrays:
        finished.append(total[at : at + a.size].reshape(a.shape))
        at += a.size
    return tuple(finished)


def cut_along(array, dim, size):
    shape = array.shape
    pieces = array.reshape(*shape[:dim], size, shape[dim] // size, *shape[dim + 1 :])
    return jnp.moveaxis(pieces, dim, 0)


def sent_and_summed(array, axis, dim):
    size = lax.axis_size(axis)
    pieces = lax.all_to_all(cut_along(array, dim, size), axis, 0, 0, tiled=True)
    return jnp.sum(pieces, axis=0)


def summed_rows(array, axes, dim):
    far, near = axes
    own = sent_and_summed(cut_along(array, dim, lax.axis_size(far)), near, dim + 1)
    return jnp.sum(lax.all_to_all(own, far, 0, 0, tiled=True), axis=0)


def padded_to(lines, size):
    spare = -len(lines) % size
    return jnp.pad(lines, [(0, spare)] + [(0, 0)] * (lines.ndim - 1))


def in_order(pieces, dim):
    shape = list(pieces.shape[1:])
    shape[dim] *= pieces.shape[0]
    return jnp.moveaxis(pieces, 0, dim).reshape(shape)


def gathered_by_axis(array, axes, dim):
    far, near = axes
    pieces = from_everyone(from_everyone(array, far), near)
    return in_order(pieces.swapaxes(0, 1).reshape(-1, *array.shape), dim)


def nested_sum(array, axes):
    own = summed_rows(padded_to(array, lax.axis_size(axes[0]) * lax.axis_size(axes[1])), axes, 0)
    whole = gathered_by_axis(own, axes, 0)
    return whole[: len(array)].reshape(array.shape)


def in_one(arrays, axis):
    ravelled, at, finished = (jnp.concatenate([a.reshape(-1) for a in arrays]), 0, [])
    total = nested_sum(ravelled, axis)
    for a in arrays:
        finished.append(total[at : at + a.size].reshape(a.shape))
        at += a.size
    return tuple(finished)


def collect(array, axis, dim):
    pieces = from_everyone(array, axis)
    return in_order(pieces, dim)


def project_twice(vec, basis, gram):
    high = lax.Precision.HIGHEST
    first, whole_sq = packed_total(
        (jnp.dot(vec, basis, precision=high), jnp.sum(vec * vec)),
        (("blk_0", "blk_1"), ("blk_2", "plane")),
    )
    coef = 2.0 * first - jnp.dot(gram, first, precision=high)
    vec = vec - jnp.dot(basis, coef, precision=high)
    total = (
        whole_sq - 2.0 * jnp.sum(coef * first) + jnp.sum(coef * jnp.dot(gram, coef, precision=high))
    )
    norm = jnp.sqrt(total + 1e-06)
    return (vec / norm, norm)


def on_device(tiles, tile_cols, tile_count, u_start, v_start, beta_start, left_basis, right_basis):
    high = lax.Precision.HIGHEST
    devices = lax.axis_size(BLK_PLANE)
    blocks, slots = tile_cols.shape
    n_tiles = v_start.shape[0] * devices // 128
    live = (lax.iota(jnp.int32, slots)[None, :] < tile_count[:, None]).astype(jnp.float32)
    onehot = (tile_cols.reshape(-1)[:, None] == lax.iota(jnp.int32, n_tiles)[None, :]).astype(
        jnp.float32
    )
    left_gram, right_gram = in_one(
        (
            jnp.dot(left_basis.T, left_basis, precision=high),
            jnp.dot(right_basis.T, right_basis, precision=high),
        ),
        (("blk_0", "blk_1"), ("blk_2", "plane")),
    )
    left_scale = math.sqrt(u_start.shape[0] * devices)
    right_scale = math.sqrt(v_start.shape[0] * devices)
    vec_right = v_start
    vec_left = u_start
    beta = beta_start[0]
    lefts, rights, coefs = ([], [], [])
    rounded = vec_right.astype(jnp.bfloat16)
    inner = collect(rounded, "plane", 0)
    whole = collect(inner, BLK, 0)
    table = whole.reshape(n_tiles, 128)
    picked = jnp.take(table, tile_cols, axis=0)
    values = jnp.einsum("rsij,rsj->rsi", tiles, picked, preferred_element_type=jnp.float32)
    forward_out = jnp.sum(values * live[:, :, None], axis=1).reshape(-1)
    vec_left, alpha = project_twice(forward_out - beta * vec_left, left_basis, left_gram)
    left_rows = vec_left.astype(jnp.bfloat16).reshape(blocks, 128)
    contrib = jnp.einsum("rsij,ri->rsj", tiles, left_rows, preferred_element_type=jnp.float32)
    contrib = (contrib * live[:, :, None]).reshape(-1, 128)
    partial_value = lax.dot_general(onehot, contrib, (((0,), (0,)), ((), ())), precision=high)
    section = summed_rows(partial_value, (("blk_0", "blk_1"), "blk_2"), 0)
    owned = sent_and_summed(section, "plane", 0)
    back_out = owned.reshape(-1)
    vec_right, beta = project_twice(back_out - alpha * vec_right, right_basis, right_gram)
    lefts.append(vec_left * left_scale)
    rights.append(vec_right * right_scale)
    coefs.append(alpha)
    coefs.append(beta)
    return (jnp.stack(lefts), jnp.stack(rights), jnp.stack(coefs))


def solution(mesh):
    torus = Mesh(
        mesh.devices.reshape(4, 8, 2, mesh.shape["plane"]), ("blk_0", "blk_1", "blk_2", "plane")
    )
    in_specs = (
        P(BLK_PLANE, None, None, None),
        P(BLK_PLANE, None),
        P(BLK_PLANE),
        P(BLK_PLANE),
        P(BLK_PLANE),
        P(),
        P(BLK_PLANE, None),
        P(BLK_PLANE, None),
    )
    out_specs = (P(None, BLK_PLANE), P(None, BLK_PLANE), P())
    return jax.shard_map(
        on_device, mesh=torus, in_specs=in_specs, out_specs=out_specs, check_vma=False
    )
```

profile of v0, /device:TPU:1, one launch (start us, length us, event | category | flops | bytes accessed | tf_op | source)
XLA Modules:
  0.0 182.7 jit_solution(4425579317650813344)
XLA Ops:
  0.6 1.8 convolution_bitcast_fusion.2
  2.4 1.4 convolution_bitcast_fusion.1
  4.5 6.6 %all-to-all-start.4 = ((f32[8,32,128]{2,1,0:T(8,128)}), f32[8,32,128]{2,1,0:T(8,128)S(1)}, u32[]{:S(2)}, u32[]{:S(2)}) async-start(f32[8,32,128]{2,1,0:T(8,128)} %maximum_bitcast_fusion), calls=%async_computation.4 | async-start | bytes 262144 | tf_op jit(solution)/shard_map/all_to_all | solution.py:45
  13.6 2.7 %all-to-all-done.4 = f32[8,32,128]{2,1,0:T(8,128)S(1)} async-done(((f32[8,32,128]{2,1,0:T(8,128)}), f32[8,32,128]{2,1,0:T(8,128)S(1)}, u32[]{:S(2)}, u32[]{:S(2)}) %all-to-all-start.4) | async-done | bytes 131104 | tf_op jit(solution)/shard_map/all_to_all | solution.py:45
  16.3 3.2 %all-to-all-start = ((bf16[4,2,128]{2,1,0:T(2,128)(2,1)}), bf16[4,2,128]{2,1,0:T(2,128)(2,1)S(1)}, u32[]{:S(2)}, u32[]{:S(2)}) async-start(bf16[4,2,128]{2,1,0:T(2,128)(2,1)} %reshape.179), calls=%async_computation | async-start | bytes 4096 | tf_op jit(solution)/shard_map/all_to_all | solution.py:15
  19.5 1.3 compare_select_fusion
  21.4 2.1 %all-to-all-done = bf16[4,2,128]{2,1,0:T(2,128)(2,1)S(1)} async-done(((bf16[4,2,128]{2,1,0:T(2,128)(2,1)}), bf16[4,2,128]{2,1,0:T(2,128)(2,1)S(1)}, u32[]{:S(2)}, u32[]{:S(2)}) %all-to-all-start) | async-done | bytes 2080 | tf_op jit(solution)/shard_map/all_to_all | solution.py:15
  24.1 10.5 %all-to-all-start.5 = ((f32[32,1,128]{2,1,0:T(1,128)}), f32[32,1,128]{2,1,0:T(1,128)S(1)}, u32[]{:S(2)}, u32[]{:S(2)}) async-start(f32[32,1,128]{2,1,0:T(1,128)} %bitcast.12), calls=%async_computation.5 | async-start | bytes 32768 | tf_op jit(solution)/shard_map/all_to_all | solution.py:52
  34.6 1.3 compare_and_fusion
  35.9 1.3 reshape.148
  38.7 2.3 %reduce.8 = bf16[64,1024]{1,0:T(8,128)(2,1)S(1)} reduce(bf16[64,1,1024]{2,1,0:T(2,128)(2,1)} %broadcast_in_dim.46, bf16[]{:T(256)} %broadcast.74), dimensions={1}, to_apply=%broadcast_in_dim.46.reduce_sub_computation | reduce | bytes 262146 | tf_op jit(solution)/shard_map/broadcast_in_dim | solution.py:14
  41.8 1.5 all-to-all-done.5
  43.3 10.3 %all-to-all-start.1 = ((bf16[64,2,512]{2,1,0:T(2,128)(2,1)}), bf16[64,2,512]{2,1,0:T(2,128)(2,1)S(1)}, u32[]{:S(2)}, u32[]{:S(2)}) async-start(bf16[64,2,512]{2,1,0:T(2,128)(2,1)} %reshape.181), calls=%async_computation.1 | async-start | bytes 262144 | tf_op jit(solution)/shard_map/all_to_all | solution.py:15
  53.6 1.2 pad_clamp_fusion
  55.5 1.3 fusion.13
  57.3 6.6 %all-to-all-done.1 = bf16[64,2,512]{2,1,0:T(2,128)(2,1)S(1)} async-done(((bf16[64,2,512]{2,1,0:T(2,128)(2,1)}), bf16[64,2,512]{2,1,0:T(2,128)(2,1)S(1)}, u32[]{:S(2)}, u32[]{:S(2)}) %all-to-all-start.1) | async-done | bytes 131104 | tf_op jit(solution)/shard_map/all_to_all | solution.py:15
  63.9 1.3 broadcast_in_dim.51
  65.2 3.9 %all-to-all-start.6 = ((f32[32,1,128]{2,1,0:T(1,128)}), f32[32,1,128]{2,1,0:T(1,128)S(1)}, u32[]{:S(2)}, u32[]{:S(2)}) async-start(f32[32,1,128]{2,1,0:T(1,128)} %broadcast_in_dim.51), calls=%async_computation.6 | async-start | bytes 32768 | tf_op jit(solution)/shard_map/all_to_all | solution.py:15
  69.9 2.3 %reduce.6 = bf16[64,1024]{1,0:T(8,128)(2,1)} reduce(bf16[64,1,1024]{2,1,0:T(2,128)(2,1)} %reshape.182, bf16[]{:T(256)} %constant.35), dimensions={1}, to_apply=%all_to_all.52.reduce_sub_computation | reduce | bytes 262146 | tf_op jit(solution)/shard_map/all_to_all | solution.py:15
  73.2 1.4 gather_fusion
  75.4 1.7 fusion.9
  79.1 8.7 %all_to_all.79 = f32[8,1,129]{2,1,0:T(1,128)} all-to-all(f32[8,1,129]{2,1,0:T(1,128)S(1)} %broadcast_in_dim.49), channel_id=1, replica_groups=mesh['blk_0'=4,'blk_1'=8,'blk_2'=2,'plane'=4] {'blk_2','plane'}, dimensions={0} | all-to-all | bytes 8256 | tf_op jit(solution)/shard_map/all_to_all | solution.py:15
  88.5 3.7 %all-to-all-start.7 = ((f32[8,32,128]{2,1,0:T(8,128)}), f32[8,32,128]{2,1,0:T(8,128)S(1)}, u32[]{:S(2)}, u32[]{:S(2)}) async-start(f32[8,32,128]{2,1,0:T(8,128)} %broadcast_in_dim.52), calls=%async_computation.7 | async-start | bytes 262144 | tf_op jit(solution)/shard_map/all_to_all | solution.py:15
  92.9 4.5 %all-to-all-done.7 = f32[8,32,128]{2,1,0:T(8,128)S(1)} async-done(((f32[8,32,128]{2,1,0:T(8,128)}), f32[8,32,128]{2,1,0:T(8,128)S(1)}, u32[]{:S(2)}, u32[]{:S(2)}) %all-to-all-start.7) | async-done | bytes 131104 | tf_op jit(solution)/shard_map/all_to_all | solution.py:15
  98.0 9.6 %all-to-all-start.3 = ((f32[32,1,129]{2,1,0:T(1,128)}), f32[32,1,129]{2,1,0:T(1,128)}, u32[]{:S(2)}, u32[]{:S(2)}) async-start(f32[32,1,129]{2,1,0:T(1,128)} %broadcast_in_dim.50), calls=%async_computation.3 | async-start | bytes 65536 | tf_op jit(solution)/shard_map/all_to_all | solution.py:15
  110.0 6.4 %all-to-all-done.3 = f32[32,1,129]{2,1,0:T(1,128)} async-done(((f32[32,1,129]{2,1,0:T(1,128)}), f32[32,1,129]{2,1,0:T(1,128)}, u32[]{:S(2)}, u32[]{:S(2)}) %all-to-all-start.3) | async-done | bytes 16544 | tf_op jit(solution)/shard_map/all_to_all | solution.py:15
  124.0 6.1 %all_to_all.80 = f32[2,32,8,128]{3,2,1,0:T(8,128)} all-to-all(f32[2,32,8,128]{3,2,1,0:T(8,128)S(1)} %copy.29), channel_id=1, replica_groups=mesh['blk_0'=4,'blk_1'=8,'blk_2'=2,'plane'=4] {'blk_2'}, dimensions={0} | all-to-all | bytes 524288 | tf_op jit(solution)/shard_map/all_to_all | solution.py:45
  131.1 12.8 %all_to_all.81 = f32[32,8,128]{2,1,0:T(8,128)} all-to-all(f32[32,8,128]{2,1,0:T(8,128)S(1)} %reduce_sum.152), channel_id=1, replica_groups=mesh['blk_0'=4,'blk_1'=8,'blk_2'=2,'plane'=4] {'blk_0','blk_1'}, dimensions={0} | all-to-all | bytes 262144 | tf_op jit(solution)/shard_map/all_to_all | solution.py:52
  144.8 6.7 %all_to_all.82 = f32[4,2,128]{2,1,0:T(2,128)S(1)} all-to-all(f32[4,2,128]{2,1,0:T(2,128)S(1)} %bitcast.133), channel_id=1, replica_groups=mesh['blk_0'=4,'blk_1'=8,'blk_2'=2,'plane'=4] {'plane'}, dimensions={0} | all-to-all | bytes 8192 | tf_op jit(solution)/shard_map/all_to_all | solution.py:45
  153.0 10.8 %all_to_all.83 = f32[8,1,129]{2,1,0:T(1,128)S(1)} all-to-all(f32[8,1,129]{2,1,0:T(1,128)S(1)} %broadcast_in_dim.53), channel_id=1, replica_groups=mesh['blk_0'=4,'blk_1'=8,'blk_2'=2,'plane'=4] {'blk_2','plane'}, dimensions={0} | all-to-all | bytes 8256 | tf_op jit(solution)/shard_map/all_to_all | solution.py:15
  164.4 3.9 %all-to-all-start.12 = ((f32[32,1,129]{2,1,0:T(1,128)}), f32[32,1,129]{2,1,0:T(1,128)S(1)}, u32[]{:S(2)}, u32[]{:S(2)}) async-start(f32[32,1,129]{2,1,0:T(1,128)} %broadcast_in_dim.54), calls=%async_computation.12 | async-start | bytes 65536 | tf_op jit(solution)/shard_map/all_to_all | solution.py:15
  168.8 8.2 %all-to-all-done.12 = f32[32,1,129]{2,1,0:T(1,128)S(1)} async-done(((f32[32,1,129]{2,1,0:T(1,128)}), f32[32,1,129]{2,1,0:T(1,128)S(1)}, u32[]{:S(2)}, u32[]{:S(2)}) %all-to-all-start.12) | async-done | bytes 16544 | tf_op jit(solution)/shard_map/all_to_all | solution.py:15
  (77 shorter events, 29.9 us)
Async XLA Ops:
  0.6 74.8 %copy-start = (bf16[4,24,128,128]{3,2,1,0:T(8,128)(2,1)S(1)}, bf16[4,24,128,128]{3,2,1,0:T(8,128)(2,1)}, u32[]{:S(2)}) copy-start(bf16[4,24,128,128]{3,2,1,0:T(8,128)(2,1)} %param.8) | copy-start | bytes 9437188
  4.5 73.4 %copy-start.1 = (f32[512,128]{1,0:T(8,128)S(1)}, f32[512,128]{1,0:T(8,128)}, u32[]{:S(2)}) copy-start(f32[512,128]{1,0:T(8,128)} %param.14) | copy-start | bytes 786436
  4.5 11.8 %all-to-all-start.4 = ((f32[8,32,128]{2,1,0:T(8,128)}), f32[8,32,128]{2,1,0:T(8,128)S(1)}, u32[]{:S(2)}, u32[]{:S(2)}) async-start(f32[8,32,128]{2,1,0:T(8,128)} %maximum_bitcast_fusion), calls=%async_computation.4 | async-start | bytes 262144 | tf_op jit(solution)/shard_map/all_to_all | solution.py:45
  16.3 7.3 %all-to-all-start = ((bf16[4,2,128]{2,1,0:T(2,128)(2,1)}), bf16[4,2,128]{2,1,0:T(2,128)(2,1)S(1)}, u32[]{:S(2)}, u32[]{:S(2)}) async-start(bf16[4,2,128]{2,1,0:T(2,128)(2,1)} %reshape.179), calls=%async_computation | async-start | bytes 4096 | tf_op jit(solution)/shard_map/all_to_all | solution.py:15
  23.6 0.6 copy-start.7
  24.1 19.1 %all-to-all-start.5 = ((f32[32,1,128]{2,1,0:T(1,128)}), f32[32,1,128]{2,1,0:T(1,128)S(1)}, u32[]{:S(2)}, u32[]{:S(2)}) async-start(f32[32,1,128]{2,1,0:T(1,128)} %bitcast.12), calls=%async_computation.5 | async-start | bytes 32768 | tf_op jit(solution)/shard_map/all_to_all | solution.py:52
  43.3 20.6 %all-to-all-start.1 = ((bf16[64,2,512]{2,1,0:T(2,128)(2,1)}), bf16[64,2,512]{2,1,0:T(2,128)(2,1)S(1)}, u32[]{:S(2)}, u32[]{:S(2)}) async-start(bf16[64,2,512]{2,1,0:T(2,128)(2,1)} %reshape.181), calls=%async_computation.1 | async-start | bytes 262144 | tf_op jit(solution)/shard_map/all_to_all | solution.py:15
  65.2 13.9 %all-to-all-start.6 = ((f32[32,1,128]{2,1,0:T(1,128)}), f32[32,1,128]{2,1,0:T(1,128)S(1)}, u32[]{:S(2)}, u32[]{:S(2)}) async-start(f32[32,1,128]{2,1,0:T(1,128)} %broadcast_in_dim.51), calls=%async_computation.6 | async-start | bytes 32768 | tf_op jit(solution)/shard_map/all_to_all | solution.py:15
  74.6 2.6 %copy-start.6 = (f32[4,24]{1,0:T(4,128)S(1)}, f32[4,24]{1,0:T(4,128)}, u32[]{:S(2)}) copy-start(f32[4,24]{1,0:T(4,128)} %fusion.13) | copy-start | bytes 1156
  74.6 2.7 %copy-start.8 = (f32[512]{0:T(512)S(1)}, f32[512]{0:T(512)}, u32[]{:S(2)}) copy-start(f32[512]{0:T(512)} %param.11) | copy-start | bytes 6148
  77.9 0.6 copy-start.5
  88.5 8.9 %all-to-all-start.7 = ((f32[8,32,128]{2,1,0:T(8,128)}), f32[8,32,128]{2,1,0:T(8,128)S(1)}, u32[]{:S(2)}, u32[]{:S(2)}) async-start(f32[8,32,128]{2,1,0:T(8,128)} %broadcast_in_dim.52), calls=%async_computation.7 | async-start | bytes 262144 | tf_op jit(solution)/shard_map/all_to_all | solution.py:15
  97.4 10.9 %copy-start.3 = (f32[8,32,128]{2,1,0:T(8,128)}, f32[8,32,128]{2,1,0:T(8,128)S(1)}, u32[]{:S(2)}) copy-start(f32[8,32,128]{2,1,0:T(8,128)S(1)} %all-to-all-done.7) | copy-start | bytes 393220
  98.0 18.4 %all-to-all-start.3 = ((f32[32,1,129]{2,1,0:T(1,128)}), f32[32,1,129]{2,1,0:T(1,128)}, u32[]{:S(2)}, u32[]{:S(2)}) async-start(f32[32,1,129]{2,1,0:T(1,128)} %broadcast_in_dim.50), calls=%async_computation.3 | async-start | bytes 65536 | tf_op jit(solution)/shard_map/all_to_all | solution.py:15
  119.7 3.9 %copy-start.4 = (s32[32,2,8]{2,1,0:T(2,128)S(1)}, s32[32,2,8]{2,1,0:T(2,128)}, u32[]{:S(2)}) copy-start(s32[32,2,8]{2,1,0:T(2,128)} %multiply_add_fusion) | copy-start | bytes 6148
  122.4 29.1 %copy-start.9 = (f32[256]{0:T(256)S(1)}, f32[256]{0:T(256)}, u32[]{:S(2)}) copy-start(f32[256]{0:T(256)} %param.12) | copy-start | bytes 3076
  122.4 29.7 %copy-start.2 = (f32[256,128]{1,0:T(8,128)S(1)}, f32[256,128]{1,0:T(8,128)}, u32[]{:S(2)}) copy-start(f32[256,128]{1,0:T(8,128)} %param.15) | copy-start | bytes 393220
  164.4 12.6 %all-to-all-start.12 = ((f32[32,1,129]{2,1,0:T(1,128)}), f32[32,1,129]{2,1,0:T(1,128)S(1)}, u32[]{:S(2)}, u32[]{:S(2)}) async-start(f32[32,1,129]{2,1,0:T(1,128)} %broadcast_in_dim.54), calls=%async_computation.12 | async-start | bytes 65536 | tf_op jit(solution)/shard_map/all_to_all | solution.py:15
where the time goes:
time: 184 us; the launch traced here: 183 us
  starting transfers between devices  51.7 us (28%)
  blocking collectives  45 us (24%)
  waiting for transfers between devices  32 us (17%)
  other arithmetic  23.7 us (13%)
  local copies, waits for them, and re-layouts  14.7 us (8%)
  matrix products  9.97 us (5%)
  between operations  5.58 us (3%)
    all_to_all x6, starting transfers between devices, from_everyone(): return lax.all_to_all(copies, axis, split_axis=0, concat_axis=0, tiled=True)  34.6 us
    all_to_all x6, waiting for transfers between devices, from_everyone(): return lax.all_to_all(copies, axis, split_axis=0, concat_axis=0, tiled=True)  27.8 us
    all_to_all x2, blocking collectives, from_everyone(): return lax.all_to_all(copies, axis, split_axis=0, concat_axis=0, tiled=True)  19.5 us
    all_to_all x1, blocking collectives, summed_rows(): return jnp.sum(lax.all_to_all(own, far, 0, 0, tiled=True), axis=0)  12.8 us
    all_to_all x2, blocking collectives, sent_and_summed(): pieces = lax.all_to_all(cut_along(array, dim, size), axis, 0, 0, tiled=True)  12.7 us
    all_to_all x1, starting transfers between devices, summed_rows(): return jnp.sum(lax.all_to_all(own, far, 0, 0, tiled=True), axis=0)  10.5 us
    all_to_all x1, starting transfers between devices, sent_and_summed(): pieces = lax.all_to_all(cut_along(array, dim, size), axis, 0, 0, tiled=True)  6.62 us
    broadcast_in_dim x9, local copies, waits for them, and re-layouts, from_everyone(): copies = jnp.broadcast_to(array, (lax.axis_size(axis), *array.shape))  4.54 us
  transfers between devices with their start and end apart: 8, of which 7 were waited for; matrix products, arithmetic and copies ran while one was open for 15% of the time, Pallas kernels for 0%

commit v1 on v0

v1 whole, which is shorter than its diff:
```python
import math

import jax
import jax.numpy as jnp
from jax import lax
from jax.experimental import pallas as pl
from jax.experimental.pallas import tpu as pltpu
from jax.sharding import PartitionSpec as P

MESH = pl.DeviceIdType.MESH
HIGH = lax.Precision.HIGHEST
F32 = jnp.float32
BF16 = jnp.bfloat16

X, Y, Z, C = 4, 4, 8, 2
PLANE = X * Y * C
BLOCKS = 4
SLOTS = 24
LANES = 32

AG_Z, AG_P, G_P, G_Z, G_ALL, C_P, C_Z, S_P, S_Z, D_P, D_Z = range(11)
EXCHANGES = 11


def high_dot(a, b):
    return jnp.dot(a, b, precision=HIGH, preferred_element_type=F32)


def gram(basis):
    return lax.dot_general(
        basis, basis, (((0,), (0,)), ((), ())), precision=HIGH, preferred_element_type=F32
    )


def kernel(
    left_scale,
    right_scale,
    tiles_h,
    cols_h,
    cnt_h,
    u_h,
    v_h,
    beta_h,
    lb_h,
    rb_h,
    out_ref,
    tiles,
    cols,
    cnt,
    beta,
    u_in,
    v_in,
    lb,
    rb,
    rowid,
    onehot,
    vz,
    vtab,
    table,
    acc_ref,
    gsend,
    g_p,
    gz_send,
    g_z,
    gp_send,
    g_all,
    ml,
    nl,
    mr,
    nr,
    c_send,
    c_p,
    cz_send,
    c_z,
    contrib,
    ub_ref,
    u_ref,
    s_send,
    s_p,
    sz_send,
    s_z,
    d_send,
    d_p,
    dz_send,
    d_z,
    local_sem,
    send_sem,
    recv_sem,
):
    blk = lax.axis_index("blk")
    x = lax.axis_index("plane")
    core = lax.rem(blk, C)
    z = lax.rem(lax.div(blk, C), Z)
    y = lax.div(blk, C * Z)
    g = y * (C * X) + core * X + x

    loads = [
        pltpu.make_async_copy(a, b, local_sem.at[i])
        for i, (a, b) in enumerate(
            [
                (v_h, v_in),
                (cols_h, cols),
                (cnt_h, cnt),
                (u_h, u_in),
                (beta_h, beta),
                (lb_h, lb),
                (rb_h, rb),
            ]
            + [(tiles_h.at[r], tiles.at[r]) for r in range(BLOCKS)]
        )
    ]
    for copy in loads:
        copy.start()

    xs = [lax.rem(x + d, X) for d in range(X)]
    ys = [lax.rem(y + d, Y) for d in range(Y)]
    cs = [lax.rem(core + d, C) for d in range(C)]
    zs = [lax.rem(z + d, Z) for d in range(Z)]
    far_x = sorted(range(X), key=lambda d: -min(d, X - d))
    far_y = sorted(range(Y), key=lambda d: -min(d, Y - d))
    plane_offsets = sorted(
        [(dx, dy, dc) for dx in far_x for dy in far_y for dc in (1, 0) if (dx, dy, dc) != (0, 0, 0)],
        key=lambda o: -(min(o[0], X - o[0]) + min(o[1], Y - o[1])),
    )
    z_offsets = sorted(range(1, Z), key=lambda d: -min(d, Z - d))

    def plane_peers():
        for dx, dy, dc in plane_offsets:
            yield (
                (ys[dy] * (Z * C) + z * C + cs[dc], xs[dx]),
                ys[dy] * (C * X) + cs[dc] * X + xs[dx],
            )

    def z_peers():
        for d in z_offsets:
            yield (y * (Z * C) + zs[d] * C + core, x), zs[d]

    def send(which, src, dst, device):
        pltpu.make_async_remote_copy(
            src_ref=src,
            dst_ref=dst,
            send_sem=send_sem.at[which],
            recv_sem=recv_sem.at[which],
            device_id=device,
            device_id_type=MESH,
        ).start()

    def arrived(which, slots, count):
        part = slots.at[pl.ds(0, count)]
        pltpu.make_async_copy(part, part, recv_sem.at[which]).wait()

    def sent(which, slots, count):
        part = slots.at[pl.ds(0, count)]
        pltpu.make_async_copy(part, part, send_sem.at[which]).wait()

    barrier = pltpu.get_barrier_semaphore()
    for device, _ in z_peers():
        pl.semaphore_signal(barrier, inc=1, device_id=device, device_id_type=MESH)
    for device, _ in plane_peers():
        pl.semaphore_signal(barrier, inc=1, device_id=device, device_id_type=MESH)

    eye = lax.broadcasted_iota(jnp.int32, (128, 128), 0) == lax.broadcasted_iota(
        jnp.int32, (128, 128), 1
    )
    diagonal = jnp.where(eye, 1.0, 0.0).astype(F32)
    for copy in loads[:7]:
        copy.wait()

    lane = lax.broadcasted_iota(jnp.int32, (1, 128), 1)
    at = jnp.full((1, 128), -1, jnp.int32)
    for r in range(BLOCKS):
        for s in range(SLOTS):
            t = cols[r, s]
            row = (t & 0x181) | ((t & 0xE) << 3) | ((t & 0x70) >> 3)
            row = jnp.where(s < cnt[r], row, PLANE * Z * 2)
            rowid[r * SLOTS + s] = row
            at = jnp.where(lane == r * LANES + s, row, at)
    onehot[...] = jnp.where(
        lax.broadcasted_iota(jnp.int32, (PLANE * Z * 2, 128), 0) == at, 1.0, 0.0
    ).astype(BF16)
    table[pl.ds(PLANE * Z * 2, 8), :] = jnp.zeros((8, 128), F32)
    contrib[...] = jnp.zeros_like(contrib)
    beta_u = u_in[...] * beta[0]
    for r in range(BLOCKS):
        acc_ref[r] = jnp.where(eye, -beta_u[r : r + 1, :], 0.0)
    vz[z] = v_in[...]
    gsend[:, 0:4, :] = gram(lb[...]).reshape(PLANE, 4, 128)
    gsend[:, 4:8, :] = gram(rb[...]).reshape(PLANE, 4, 128)

    pl.semaphore_wait(barrier, PLANE - 1 + Z - 1)

    for device, _ in z_peers():
        send(AG_Z, v_in, vz.at[z], device)
    for device, peer in plane_peers():
        send(G_P, gsend.at[peer], g_p.at[g], device)
    g_p[g] = gsend[g]
    arrived(AG_Z, vz, Z - 1)
    vtab[g] = vz[...].reshape(2 * Z, 128).astype(BF16)
    for device, _ in plane_peers():
        send(AG_P, vtab.at[g], vtab.at[g], device)
    arrived(G_P, g_p, PLANE - 1)
    gz = jnp.sum(g_p[...], axis=0)
    gz_send[...] = gz
    g_z[z] = gz
    for device, _ in z_peers():
        send(G_Z, gz_send, g_z.at[z], device)
    for copy in loads[7:]:
        copy.wait()
    arrived(AG_P, vtab, PLANE - 1)
    table[pl.ds(0, PLANE * Z * 2), :] = vtab[...].astype(F32).reshape(PLANE * Z * 2, 128)

    ps = []
    for r in range(BLOCKS):

        def forward(s, acc, r=r):
            row = table[pl.ds(rowid[r * SLOTS + s], 1), :]
            return acc + tiles[r, s].astype(F32) * row

        acc = lax.fori_loop(0, SLOTS, forward, acc_ref[r], unroll=4)
        ps.append(jnp.broadcast_to(jnp.sum(acc, axis=1, keepdims=True), (128, 128)))

    def inner(basis_rows, columns):
        first = sum(
            jnp.sum(b * c, axis=0, keepdims=True) for b, c in zip(basis_rows, columns)
        )
        square = sum(jnp.sum(c * c, axis=0, keepdims=True) for c in columns)
        return first, square

    def total(slots):
        return jnp.sum(slots[...], axis=0)

    first, square = inner([lb[pl.ds(r * 128, 128), :] for r in range(BLOCKS)], ps)
    c_send[0:1, :] = first
    c_send[1:2, :] = square
    c_p[g] = c_send[...]
    for device, _ in plane_peers():
        send(C_P, c_send, c_p.at[g], device)
    for r in range(BLOCKS):
        acc_ref[r] = ps[r]
    arrived(G_Z, g_z, Z - 1)
    gp = jnp.sum(g_z[...], axis=0)
    gp_send[...] = gp
    g_all[g] = gp
    for device, _ in plane_peers():
        send(G_ALL, gp_send, g_all.at[g], device)
    arrived(C_P, c_p, PLANE - 1)
    cz = total(c_p)
    cz_send[...] = cz
    c_z[z] = cz
    for device, _ in z_peers():
        send(C_Z, cz_send, c_z.at[z], device)
    arrived(G_ALL, g_all, PLANE - 1)
    left_gram = g_all[:, 0:4, :].reshape(128, 128)
    right_gram = g_all[:, 4:8, :].reshape(128, 128)

    def twice(gram_matrix):
        b = 2.0 * diagonal - gram_matrix
        return b, 2.0 * b - high_dot(b, high_dot(gram_matrix, b))

    bl, nl[...] = twice(left_gram)
    ml[...] = high_dot(lb[...], bl)

    def norm_of(first, square, quadratic):
        column = jnp.sum(quadratic * first, axis=1, keepdims=True)
        inner_sum = jnp.sum(jnp.where(eye, column, 0.0) * first, axis=0, keepdims=True)
        inner_sum = jnp.sum(inner_sum, axis=1, keepdims=True)
        return jnp.sqrt(square - inner_sum + 1e-6)

    arrived(C_Z, c_z, Z - 1)
    both = total(c_z)
    first, square = both[0:1, :], both[1:2, :]
    alpha = norm_of(first, square, nl[...])
    contribs = []
    for r in range(BLOCKS):
        less = jnp.sum(ml[pl.ds(r * 128, 128), :] * first, axis=1, keepdims=True)
        u = (acc_ref[r] - less) / alpha
        u_ref[r] = u
        ub_ref[r] = u.astype(BF16).astype(F32)
    for r in range(BLOCKS):

        def backward(s, _, r=r):
            part = jnp.sum(tiles[r, s].astype(F32) * ub_ref[r], axis=0, keepdims=True)
            contrib[pl.ds(r * LANES + s, 1), :] = part
            return 0

        lax.fori_loop(0, SLOTS, backward, 0, unroll=4)
    whole = contrib[...]
    high = whole.astype(BF16)
    rest = whole - high.astype(F32)
    middle = rest.astype(BF16)
    low = (rest - middle.astype(F32)).astype(BF16)
    hot = onehot[...]
    partial = (
        jnp.dot(hot, high, preferred_element_type=F32)
        + jnp.dot(hot, middle, preferred_element_type=F32)
        + jnp.dot(hot, low, preferred_element_type=F32)
    )
    s_send[...] = partial.reshape(PLANE, 2 * Z, 128)
    for device, peer in plane_peers():
        send(S_P, s_send.at[peer], s_p.at[g], device)
    s_p[g] = s_send[g]
    for r in range(BLOCKS):
        out_ref[r : r + 1, :] = left_scale * jnp.sum(
            jnp.where(eye, u_ref[r], 0.0), axis=0, keepdims=True
        )
    br, nr[...] = twice(right_gram)
    mr[...] = high_dot(rb[...], br)
    arrived(S_P, s_p, PLANE - 1)
    sz_send[...] = total(s_p).reshape(Z, 2, 128)
    s_z[z] = sz_send[z]
    for device, peer in z_peers():
        send(S_Z, sz_send.at[peer], s_z.at[z], device)
    arrived(S_Z, s_z, Z - 1)
    residual = total(s_z) - alpha * v_in[...]
    rs = [
        jnp.broadcast_to(
            jnp.sum(jnp.where(eye, residual[h : h + 1, :], 0.0), axis=1, keepdims=True), (128, 128)
        )
        for h in range(2)
    ]
    first, square = inner([rb[pl.ds(h * 128, 128), :] for h in range(2)], rs)
    d_send[0:1, :] = first
    d_send[1:2, :] = square
    d_p[g] = d_send[...]
    for device, _ in plane_peers():
        send(D_P, d_send, d_p.at[g], device)
    arrived(D_P, d_p, PLANE - 1)
    dz = total(d_p)
    dz_send[...] = dz
    d_z[z] = dz
    for device, _ in z_peers():
        send(D_Z, dz_send, d_z.at[z], device)
    arrived(D_Z, d_z, Z - 1)
    both = total(d_z)
    first, square = both[0:1, :], both[1:2, :]
    new_beta = norm_of(first, square, nr[...])
    for h in range(2):
        less = jnp.sum(mr[pl.ds(h * 128, 128), :] * first, axis=1, keepdims=True)
        v = (rs[h] - less) / new_beta
        out_ref[4 + h : 5 + h, :] = right_scale * jnp.sum(
            jnp.where(eye, v, 0.0), axis=0, keepdims=True
        )
    out_ref[6:7, :] = jnp.where(lane == 0, alpha, new_beta)
    out_ref[7:8, :] = jnp.zeros((1, 128), F32)

    for which, slots, count in (
        (AG_Z, vz, Z - 1),
        (AG_P, vtab, PLANE - 1),
        (G_P, g_p, PLANE - 1),
        (G_Z, g_z, Z - 1),
        (G_ALL, g_all, PLANE - 1),
        (C_P, c_p, PLANE - 1),
        (C_Z, c_z, Z - 1),
        (S_P, s_p, PLANE - 1),
        (S_Z, s_z, Z - 1),
        (D_P, d_p, PLANE - 1),
        (D_Z, d_z, Z - 1),
    ):
        sent(which, slots, count)


def solution(mesh):
    devices = math.prod(mesh.shape.values())

    def step(tiles, tile_cols, tile_count, u_start, v_start, beta_start, left_basis, right_basis):
        vmem = pltpu.VMEM
        out = pl.pallas_call(
            lambda *refs: kernel(
                math.sqrt(u_start.shape[0] * devices), math.sqrt(v_start.shape[0] * devices), *refs
            ),
            name="lanczos_step",
            out_shape=jax.ShapeDtypeStruct((8, 128), F32),
            in_specs=[pl.BlockSpec(memory_space=pl.ANY)] * 8,
            out_specs=pl.BlockSpec(memory_space=pltpu.VMEM),
            scratch_shapes=[
                vmem((BLOCKS, SLOTS, 128, 128), BF16),
                pltpu.SMEM((BLOCKS, SLOTS), jnp.int32),
                pltpu.SMEM((BLOCKS,), jnp.int32),
                pltpu.SMEM((1,), F32),
                vmem((BLOCKS, 128), F32),
                vmem((2, 128), F32),
                vmem((BLOCKS * 128, 128), F32),
                vmem((2 * 128, 128), F32),
                pltpu.SMEM((BLOCKS * SLOTS,), jnp.int32),
                vmem((PLANE * Z * 2, 128), BF16),
                vmem((Z, 2, 128), F32),
                vmem((PLANE, 2 * Z, 128), BF16),
                vmem((PLANE * Z * 2 + 8, 128), F32),
                vmem((BLOCKS, 128, 128), F32),
                vmem((PLANE, 8, 128), F32),
                vmem((PLANE, 8, 128), F32),
                vmem((8, 128), F32),
                vmem((Z, 8, 128), F32),
                vmem((8, 128), F32),
                vmem((PLANE, 8, 128), F32),
                vmem((BLOCKS * 128, 128), F32),
                vmem((128, 128), F32),
                vmem((2 * 128, 128), F32),
                vmem((128, 128), F32),
                vmem((2, 128), F32),
                vmem((PLANE, 2, 128), F32),
                vmem((2, 128), F32),
                vmem((Z, 2, 128), F32),
                vmem((128, 128), F32),
                vmem((BLOCKS, 128, 128), F32),
                vmem((BLOCKS, 128, 128), F32),
                vmem((PLANE, 2 * Z, 128), F32),
                vmem((PLANE, 2 * Z, 128), F32),
                vmem((Z, 2, 128), F32),
                vmem((Z, 2, 128), F32),
                vmem((2, 128), F32),
                vmem((PLANE, 2, 128), F32),
                vmem((2, 128), F32),
                vmem((Z, 2, 128), F32),
                pltpu.SemaphoreType.DMA((7 + BLOCKS,)),
                pltpu.SemaphoreType.DMA((EXCHANGES,)),
                pltpu.SemaphoreType.DMA((EXCHANGES,)),
            ],
            compiler_params=pltpu.CompilerParams(collective_id=0, has_side_effects=True),
        )(
            tiles,
            tile_cols,
            tile_count,
            u_start.reshape(BLOCKS, 128),
            v_start.reshape(2, 128),
            beta_start,
            left_basis,
            right_basis,
        )
        return out[0:4].reshape(1, -1), out[4:6].reshape(1, -1), out[6, 0:2]

    both = ("blk", "plane")
    return jax.shard_map(
        step,
        mesh=mesh,
        in_specs=(
            P(both, None, None, None),
            P(both, None),
            P(both),
            P(both),
            P(both),
            P(),
            P(both, None),
            P(both, None),
        ),
        out_specs=(P(None, both), P(None, both), P()),
        check_vma=False,
    )
```

time: 184 us -> 56.1 us (0.30)
  starting transfers between devices: 51.7 us -> 0 us
  Pallas kernels: 0 us -> 50.9 us
  blocking collectives: 45 us -> 0 us
  waiting for transfers between devices: 32 us -> 0 us
  other arithmetic: 23.7 us -> 0 us
  local copies, waits for them, and re-layouts: 14.7 us -> 3.7 us
  matrix products: 9.97 us -> 0 us
  between operations: 5.58 us -> 1.29 us
    all_to_all x8 -> x0, starting transfers between devices: 51.7 us -> none  [the longest x6 34.6 us: from_everyone(): return lax.all_to_all(copies, axis, split_axis=0, concat_axis=0, tiled=True)]
    pallas_call x0 -> x1, Pallas kernels: none -> 50.9 us  [step(): pl.pallas_call(lambda *refs: kernel(math.sqrt(u_start.shape[0] * devices)...]
    all_to_all x5 -> x0, blocking collectives: 45 us -> none  [the longest x2 19.5 us: from_everyone(): return lax.all_to_all(copies, axis, split_axis=0, concat_axis=0, tiled=True)]
    all_to_all x8 -> x0, waiting for transfers between devices: 32 us -> none  [the longest x6 27.8 us: from_everyone(): return lax.all_to_all(copies, axis, split_axis=0, concat_axis=0, tiled=True)]
    dot_general x13 -> x0, matrix products: 9.97 us -> none  [the longest x1 1.77 us: on_device(): jnp.dot(left_basis.T, left_basis, precision=high)]
    reduce_sum x12 -> x0, other arithmetic: 6.03 us -> none  [the longest x4 1.61 us: of_everyone(): return from_everyone(array, axis).sum(axis=0)]
    broadcast_in_dim x10 -> x0, local copies, waits for them, and re-layouts: 5.82 us -> none  [the longest x9 4.54 us: from_everyone(): copies = jnp.broadcast_to(array, (lax.axis_size(axis), *array.shape))]
    unnamed x25 -> x0, local copies, waits for them, and re-layouts: 3.73 us -> none
  transfers between devices with their start and end apart: 8 -> 0, of which waited for: 7 -> 0; matrix products, arithmetic and copies ran while one was open for 15% -> 0% of each run, Pallas kernels for 0% -> 0%
where the time goes in v1:
time: 56.1 us; the launch traced here: 55.9 us
  Pallas kernels  50.9 us (91%)
  local copies, waits for them, and re-layouts  3.7 us (7%)
  between operations  1.29 us (2%)
    pallas_call x1, Pallas kernels, step(): pl.pallas_call(lambda *refs: kernel(math.sqrt(u_start.shape[0] * devices)...  50.9 us
    slice x2, local copies, waits for them, and re-layouts, step(): return (out[0:4].reshape(1, -1), out[4:6].reshape(1, -1), out[6, 0:2])  2.5 us
    squeeze x1, local copies, waits for them, and re-layouts, step(): return (out[0:4].reshape(1, -1), out[4:6].reshape(1, -1), out[6, 0:2])  1.2 us

profile of v1, /device:TPU:1, one launch (start us, length us, event | category | flops | bytes accessed | tf_op | source)
XLA Modules:
  0.0 55.9 jit_solution(12401345967593484087)
XLA Ops:
  1.3 50.9 %lanczos_step.1 = f32[8,128]{1,0:T(8,128)} custom-call(bf16[4,24,128,128]{3,2,1,0:T(8,128)(2,1)} %refs_0_.1, s32[4,24]{1,0:T(4,128)} %refs_1_.1, s32[4]{0:T(128)} %refs_2_.1, f32[4,128]{1,0:T(4,128)} %bitcast.6, f32[2,128]{1,0:T(2,128)} %bitcast.8, f32[1]{0:T(128)S(6)} %copy.11.refs_5_, f32[512,128]{1,0:T(8,128)} %refs_6_.1, f32[256,128]{1,0:T(8,128)} %refs_7_.1), custom_call_target="tpu_custom_call" | custom-call | tf_op jit(solution)/shard_map/lanczos_step/pallas_call | solution.py:367
  52.2 1.2 %slice_bitcast_fusion = f32[2]{0:T(128)} fusion(f32[8,128]{1,0:T(8,128)} %lanczos_step.1), kind=kLoop, calls=%fused_computation | loop fusion | bytes 16 | tf_op jit(solution)/shard_map/squeeze | solution.py:430
  53.4 1.2 %slice.10 = f32[2,128]{1,0:T(2,128)} slice(f32[8,128]{1,0:T(8,128)} %lanczos_step.1), slice={[4:6], [0:128]} | slice | bytes 2048 | tf_op jit(solution)/shard_map/slice | solution.py:430
  54.6 1.3 %slice.9 = f32[4,128]{1,0:T(4,128)} slice(f32[8,128]{1,0:T(8,128)} %lanczos_step.1), slice={[0:4], [0:128]} | slice | bytes 4096 | tf_op jit(solution)/shard_map/slice | solution.py:430

commit v2 on v1

--- a/solution.py
+++ b/solution.py
@@ -147,7 +147,8 @@
 
     def arrived(which, slots, count):
         part = slots.at[pl.ds(0, count)]
-        pltpu.make_async_copy(part, part, recv_sem.at[which]).wait()
+        with jax.named_scope(f"wait_{which}"):
+            pltpu.make_async_copy(part, part, recv_sem.at[which]).wait()
 
     def sent(which, slots, count):
         part = slots.at[pl.ds(0, count)]
@@ -163,8 +164,9 @@
         jnp.int32, (128, 128), 1
     )
     diagonal = jnp.where(eye, 1.0, 0.0).astype(F32)
-    for copy in loads[:7]:
-        copy.wait()
+    with jax.named_scope("wait_small"):
+        for copy in loads[:7]:
+            copy.wait()
 
     lane = lax.broadcasted_iota(jnp.int32, (1, 128), 1)
     at = jnp.full((1, 128), -1, jnp.int32)
@@ -180,14 +182,15 @@
     ).astype(BF16)
     table[pl.ds(PLANE * Z * 2, 8), :] = jnp.zeros((8, 128), F32)
     contrib[...] = jnp.zeros_like(contrib)
-    beta_u = u_in[...] * beta[0]
+    beta_u = u_in[...] * beta[...]
     for r in range(BLOCKS):
         acc_ref[r] = jnp.where(eye, -beta_u[r : r + 1, :], 0.0)
     vz[z] = v_in[...]
     gsend[:, 0:4, :] = gram(lb[...]).reshape(PLANE, 4, 128)
     gsend[:, 4:8, :] = gram(rb[...]).reshape(PLANE, 4, 128)
 
-    pl.semaphore_wait(barrier, PLANE - 1 + Z - 1)
+    with jax.named_scope("wait_barrier"):
+        pl.semaphore_wait(barrier, PLANE - 1 + Z - 1)
 
     for device, _ in z_peers():
         send(AG_Z, v_in, vz.at[z], device)
@@ -204,8 +207,9 @@
     g_z[z] = gz
     for device, _ in z_peers():
         send(G_Z, gz_send, g_z.at[z], device)
-    for copy in loads[7:]:
-        copy.wait()
+    with jax.named_scope("wait_tiles"):
+        for copy in loads[7:]:
+            copy.wait()
     arrived(AG_P, vtab, PLANE - 1)
     table[pl.ds(0, PLANE * Z * 2), :] = vtab[...].astype(F32).reshape(PLANE * Z * 2, 128)
 
@@ -359,6 +363,13 @@
         sent(which, slots, count)
 
 
+def finish(out, left, right, coefs):
+    left[...] = out[0:BLOCKS, :]
+    right[...] = out[BLOCKS : BLOCKS + 2, :]
+    coefs[0] = out[6, 0]
+    coefs[1] = out[6, 1]
+
+
 def solution(mesh):
     devices = math.prod(mesh.shape.values())
 
@@ -369,14 +380,14 @@
                 math.sqrt(u_start.shape[0] * devices), math.sqrt(v_start.shape[0] * devices), *refs
             ),
             name="lanczos_step",
-            out_shape=jax.ShapeDtypeStruct((8, 128), F32),
-            in_specs=[pl.BlockSpec(memory_space=pl.ANY)] * 8,
+            out_shape=pltpu.VMEM((8, 128), F32),
+            in_specs=[pl.BlockSpec(memory_space=pltpu.HBM)] * 8,
             out_specs=pl.BlockSpec(memory_space=pltpu.VMEM),
             scratch_shapes=[
                 vmem((BLOCKS, SLOTS, 128, 128), BF16),
                 pltpu.SMEM((BLOCKS, SLOTS), jnp.int32),
                 pltpu.SMEM((BLOCKS,), jnp.int32),
-                pltpu.SMEM((1,), F32),
+                vmem((1, 1), F32),
                 vmem((BLOCKS, 128), F32),
                 vmem((2, 128), F32),
                 vmem((BLOCKS * 128, 128), F32),
@@ -416,18 +427,36 @@
                 pltpu.SemaphoreType.DMA((EXCHANGES,)),
                 pltpu.SemaphoreType.DMA((EXCHANGES,)),
             ],
-            compiler_params=pltpu.CompilerParams(collective_id=0, has_side_effects=True),
+            compiler_params=pltpu.CompilerParams(
+                collective_id=0, has_side_effects=True
+            ),
         )(
             tiles,
             tile_cols,
             tile_count,
             u_start.reshape(BLOCKS, 128),
             v_start.reshape(2, 128),
-            beta_start,
+            beta_start.reshape(1, 1),
             left_basis,
             right_basis,
         )
-        return out[0:4].reshape(1, -1), out[4:6].reshape(1, -1), out[6, 0:2]
+        left, right, coefs = pl.pallas_call(
+            finish,
+            name="finish",
+            out_shape=(
+                jax.ShapeDtypeStruct((BLOCKS, 128), F32),
+                jax.ShapeDtypeStruct((2, 128), F32),
+                jax.ShapeDtypeStruct((2,), F32),
+            ),
+            in_specs=[pl.BlockSpec(memory_space=pltpu.VMEM)],
+            out_specs=(
+                pl.BlockSpec(memory_space=pltpu.VMEM),
+                pl.BlockSpec(memory_space=pltpu.VMEM),
+                pl.BlockSpec(memory_space=pltpu.SMEM),
+            ),
+            compiler_params=pltpu.CompilerParams(vmem_limit_bytes=1 << 20),
+        )(out)
+        return left.reshape(1, -1), right.reshape(1, -1), coefs
 
     both = ("blk", "plane")
     return jax.shard_map(

time: 56.1 us -> 52.3 us (0.932)
  local copies, waits for them, and re-layouts: 3.7 us -> 0 us
    slice x2 -> x0, local copies, waits for them, and re-layouts: 2.5 us -> none  [step(): return (out[0:4].reshape(1, -1), out[4:6].reshape(1, -1), out[6, 0:2])]
    squeeze x1 -> x0, local copies, waits for them, and re-layouts: 1.2 us -> none  [step(): return (out[0:4].reshape(1, -1), out[4:6].reshape(1, -1), out[6, 0:2])]
    pallas_call x0 -> x1, Pallas kernels: none -> 0.62 us  [step(): pl.pallas_call(finish, name='finish', out_shape=(jax.ShapeDtypeStruct((BL...]
    pallas_call x1, Pallas kernels: 50.9 us -> 50.3 us  [step(): pl.pallas_call(lambda *refs: kernel(math.sqrt(u_start.shape[0] * devices)...]
where the time goes in v2:
time: 52.3 us; the launch traced here: 52.2 us
  Pallas kernels  50.9 us (97%)
  between operations  1.29 us (2%)
    pallas_call x1, Pallas kernels, step(): pl.pallas_call(lambda *refs: kernel(math.sqrt(u_start.shape[0] * devices)...  50.3 us

profile of v2, /device:TPU:1, one launch (start us, length us, event | category | flops | bytes accessed | tf_op | source)
XLA Modules:
  0.0 52.2 jit_solution(5681335011525929961)
XLA Ops:
  1.3 50.3 %lanczos_step.1.out = f32[8,128]{1,0:T(8,128)S(1)} custom-call(bf16[4,24,128,128]{3,2,1,0:T(8,128)(2,1)} %refs_0_.1, s32[4,24]{1,0:T(4,128)} %refs_1_.1, s32[4]{0:T(128)} %refs_2_.1, f32[4,128]{1,0:T(4,128)} %bitcast.6, f32[2,128]{1,0:T(2,128)} %bitcast.7, f32[1,1]{1,0:T(1,128)} %bitcast.5.refs_5_, f32[512,128]{1,0:T(8,128)} %refs_6_.1, f32[256,128]{1,0:T(8,128)} %refs_7_.1), custom_call_target="tpu_custom_call" | custom-call | tf_op jit(solution)/shard_map/lanczos_step/pallas_call | solution.py:378
  51.6 0.6 %finish.1 = (f32[4,128]{1,0:T(4,128)}, f32[2,128]{1,0:T(2,128)}, f32[2]{0:T(128)}) custom-call(f32[8,128]{1,0:T(8,128)S(1)} %lanczos_step.1.out), custom_call_target="tpu_custom_call" | custom-call | tf_op jit(solution)/shard_map/finish/pallas_call | solution.py:443
